TPU v7x, 32 devices: a whole 2x2x4 slice. The times are simulated.
32 devices in a mesh: lat: 2 (over y), lon: 8 (over z, x), lev: 2 (over core).
Axes of the slice: x: 2, y: 2, z: 4, core: 2. Of those that a mesh axis runs over, the one named last changes fastest.
Arguments:
- tokens: bfloat16 [4, 12, 96, 192], P('lev', 'lat', 'lon'), may hold values from -6 to 6
- norm1_gain: float32 [192], replicated, may hold values from 0.8 to 10
- qkv_weight: bfloat16 [192, 576], replicated, may hold values from -0.4375 to 0.4375
- proj_weight: bfloat16 [192, 192], replicated, may hold values from -0.4375 to 0.4375
- earth_bias: bfloat16 [2, 2, 6, 3312], P(None, 'lat'), may hold values from -4 to 4
- norm2_gain: float32 [192], replicated, may hold values from 0.5 to 1.5
- fc1_weight: bfloat16 [192, 768], replicated, may hold values from -0.4375 to 0.4375
- fc2_weight: bfloat16 [768, 192], replicated, may hold values from -0.21875 to 0.21875
Outputs:
- blended: bfloat16 [4, 12, 96, 192], P('lev', 'lat', 'lon')
All inputs are finite; a program needn't handle non-finite values.
Results may differ from a plain program's by a relative error of at most 0.008.
The roundings to bfloat16 on the way count: a program that leaves them out, or rounds other values in their place, can miss the bound.
Values may be sent and summed in bfloat16 or wider, within the bound.
A program may use at most 64 MiB of HBM per device.

v0:
```python
import functools

import jax
import jax.numpy as jnp
import numpy as np
from jax import lax
from jax.experimental import pallas as pl
from jax.experimental.pallas import tpu as pltpu
from jax.sharding import PartitionSpec as P

HEADS = 6
WLV = 2
WLA = 6
WLO = 12
HALF_LA = WLA // 2
HALF_LO = WLO // 2
OCT = HALF_LA * HALF_LO
PITCH = 24
SIDE = 2 * PITCH
LATS = 2 * SIDE
SPAN = 2 * WLO - 1
CHUNK = WLA * SPAN
ROWS = 8
LANES = 128
AXES = ("lev", "lat", "lon")
OPERANDS = 9
STACK = HEADS * PITCH
SECTION = HALF_LA * CHUNK
KINDS = 5

norm_eps = 1e-05


def octant_row(lat, lon):
    return lat // HALF_LA * PITCH + lat % HALF_LA * HALF_LO + lon % HALF_LO


def toeplitz_matrix():
    pick = np.zeros((CHUNK, WLO * LANES), np.float32)
    for lon in range(WLO):
        for key_lat in range(WLA):
            for key_lon in range(WLO):
                column = lon * LANES + key_lon // HALF_LO * SIDE + octant_row(key_lat, key_lon)
                pick[key_lat * SPAN + lon - key_lon + WLO - 1, column] = 1
    return pick


def layer_norm(values, scale_gain):
    average = jnp.mean(values, axis=-1, keepdims=True)
    centered = values - average
    variance = jnp.mean(centered * centered, axis=-1, keepdims=True)
    return centered * lax.rsqrt(variance + norm_eps) * scale_gain


def matmul(a, b):
    return jnp.dot(a, b, preferred_element_type=jnp.float32)


def lat_moves(size, at):
    stay = (0, PITCH, PITCH, SIDE)
    if size == 2:
        source = pl.multiple_of((2 - at) * PITCH, PITCH)
        target = pl.multiple_of(at * 3 * PITCH, PITCH)
        return (stay, (1, source, target, PITCH))
    return (stay, (1, 2 * PITCH, 0, PITCH), (-1, PITCH, 3 * PITCH, PITCH))


def lon_moves():
    return (
        (1, slice(2, 3), slice(0, 1)),
        (-1, slice(1, 2), slice(3, 4)),
        (0, slice(1, 3), slice(1, 3)),
    )


def message_count(sizes):
    lats = len(lat_moves(sizes[1], 0))
    return 4 * lats + (lats - 1) + 3 + 1


def kernel(sizes, *refs):
    operands, out_ref, held = refs[:OPERANDS], refs[OPERANDS], refs[OPERANDS + 1 : -14]
    (
        own,
        cells,
        tables,
        chunks_out,
        chunks_in,
        bias,
        weights,
        stacked,
        keys,
        values,
        rows_out,
        sems,
        load_sems,
        ready,
    ) = refs[-14:]
    loads = [
        pltpu.make_async_copy(source, place, load_sems.at[i])
        for i, (source, place) in enumerate(zip(operands, held))
    ]
    for load in loads:
        load.start()
    (
        tokens_ref,
        gain1_ref,
        table_ref,
        pick_ref,
        qkv_ref,
        proj_ref,
        gain2_ref,
        fc1_ref,
        fc2_ref,
    ) = held
    lev, lat, lon = where = [lax.axis_index(axis) for axis in AXES]
    features = own.shape[-1]
    slots = (lev, 1 - lev)

    def device(steps):
        return {
            axis: lax.rem(at + step + size, size)
            for axis, at, step, size in zip(AXES, where, steps, sizes)
        }

    moves = lat_moves(sizes[1], lat)
    per_side = 2 * len(moves)

    def remote(source, target, index, there):
        return pltpu.make_async_remote_copy(
            src_ref=source,
            dst_ref=target,
            send_sem=sems.at[0, index],
            recv_sem=sems.at[1, index],
            device_id=there,
            device_id_type=pl.DeviceIdType.MESH,
        )

    tail_kinds, plain_kind = slice(1, 3), slice(0, 1)
    first_parts, last_parts, peers = {}, {}, {}
    for side, (lon_step, lon_from, lon_to) in enumerate(lon_moves()[:2]):
        first_parts[lon_step], last_parts[lon_step], peers[lon_step] = [], [], []
        for at, (lat_step, lat_from, lat_to, rows) in enumerate(moves):
            there = device((0, lat_step, lon_step))
            peers[lon_step].append(there)
            for part, kinds in enumerate((tail_kinds, plain_kind)):
                (first_parts, last_parts)[part][lon_step].append(
                    remote(
                        cells.at[lon_from, kinds, pl.ds(lat_from, rows), :],
                        cells.at[lon_to, kinds, pl.ds(lat_to, rows), :],
                        side * per_side + at * 2 + part,
                        there,
                    )
                )
    row_copies, row_peers = [], []
    for at, (lat_step, lat_from, lat_to, rows) in enumerate(moves[1:]):
        row_peers.append(device((0, lat_step, 0)))
        row_copies.append(
            remote(
                cells.at[1:3, 0:3, pl.ds(lat_from, rows), :],
                cells.at[1:3, 0:3, pl.ds(lat_to, rows), :],
                2 * per_side + at,
                row_peers[-1],
            )
        )
    partner = device((1, 0, 0))
    passed = 2 * per_side + len(row_copies)

    def pass_on(columns, index):
        return remote(
            cells.at[columns, 1:3, :, :], cells.at[columns, 3:5, :, :], passed + index, partner
        )

    own_pass = pass_on(slice(1, 3), 2)
    table_copy = remote(chunks_out, chunks_in, passed + 3, device((0, 1, 0)))

    barrier = pltpu.get_barrier_semaphore()
    first_lon, last_lon = lon == 0, lon == sizes[2] - 1

    def tell(semaphore, group):
        for there in group:
            pl.semaphore_signal(
                semaphore, inc=1, device_id=there, device_id_type=pl.DeviceIdType.MESH
            )

    tell(barrier, row_peers + [partner] + peers[-1])
    pl.when(jnp.logical_not(last_lon))(lambda: tell(barrier, peers[1]))
    wrapped = len(moves)
    greetings = len(row_peers) + 1 + 2 * wrapped

    for start in (OCT, PITCH + OCT):
        own[:, :, start : start + PITCH - OCT, :] = jnp.zeros(
            (2, 2, PITCH - OCT, features), jnp.float32
        )
    if sizes[1] == 2:
        blank = jnp.zeros((4, 3, PITCH, LANES), jnp.bfloat16)

        def clear_low():
            cells[:, 0:3, :PITCH, :] = blank

        def clear_high():
            cells[:, 0:3, 3 * PITCH :, :] = blank

        pl.when(lat == 0)(clear_low)
        pl.when(lat == 1)(clear_high)

    loads[0].wait()
    for a in range(WLA):
        for o in range(WLO):
            cell = tokens_ref[a, o].astype(jnp.float32)
            row = octant_row(a, o)
            for side in range(WLV):
                own[o // HALF_LO, slots[side], row : row + 1, :] = cell[side : side + 1]
    loads[1].wait()
    normed = layer_norm(own[...].reshape(4 * SIDE, features), gain1_ref[...])
    for half in range(2):
        plain = normed[half * 2 * SIDE : half * 2 * SIDE + SIDE]
        paired = normed[half * 2 * SIDE + SIDE : (half + 1) * 2 * SIDE]
        tails = jnp.concatenate([plain[:, LANES:], paired[:, LANES:]], axis=1)
        for kind, block in enumerate((plain[:, :LANES], paired[:, :LANES], tails)):
            cells[1 + half, kind, PITCH : PITCH + SIDE, :] = block.astype(jnp.bfloat16)
    normed = normed.astype(jnp.bfloat16)
    pl.semaphore_wait(barrier, jnp.where(first_lon, greetings - wrapped, greetings))

    def start(*groups):
        for group in groups:
            for copy in group:
                copy.start()

    def start_side(lon_step):
        start(first_parts[lon_step], last_parts[lon_step])

    @pl.when(last_lon)
    def _():
        if sizes[1] == 2:
            for at_lat in range(2):

                @pl.when(lat == at_lat)
                def _(at_lat=at_lat):
                    for to_lat in range(2):
                        first_parts[1][at_lat ^ to_lat].start()
                        last_parts[1][at_lat ^ to_lat].start()
        else:
            start_side(1)
        tell(ready, peers[1])
        start_side(-1)

    pl.when(first_lon)(lambda: start_side(1))

    @pl.when(jnp.logical_not(first_lon | last_lon))
    def _():
        start(first_parts[1], first_parts[-1], last_parts[1], last_parts[-1])

    start(row_copies)

    loads[2].wait()
    tables[...] = jnp.zeros_like(tables)
    for head in range(HEADS):
        pair = table_ref[0, head].astype(jnp.float32)
        for kind in range(WLV):
            tables[kind, head : head + 1, :] = pair[kind : kind + 1]

    def section(kind, query_lev, key_lev, side):
        at = (query_lev * WLV + key_lev) * WLA * CHUNK + side * SECTION
        return tables[kind, :, at : at + SECTION]

    def sections(side):
        found = [
            jnp.where(lev == 0, section(kind, *low, side), section(kind, *high, side))
            for kind, low, high in ((1, (1, 1), (0, 0)), (0, (0, 0), (1, 1)), (0, (0, 1), (1, 0)))
        ]
        return jnp.concatenate(found, axis=0)

    chunks_out[...] = sections(1).astype(jnp.bfloat16)
    table_copy.start()
    own_chunks = sections(0)

    lane = lax.broadcasted_iota(jnp.int32, (ROWS, LANES), 1)
    lat_side = lane % SIDE // PITCH
    real = (lane < LATS) & (lane % PITCH < OCT)
    partner_out = (lat == 0, lat == sizes[1] - 1)

    def fill_bias(half, found):
        chunk_rows = jnp.concatenate(
            [found[:, step * CHUNK : (step + 1) * CHUNK] for step in range(HALF_LA)], axis=0
        )
        spread = matmul(chunk_rows.astype(jnp.bfloat16), pick_ref[...])
        allowed = real & ((lat_side != half) | jnp.logical_not(partner_out[half]))
        for step in range(HALF_LA):
            for kind in range(3):
                at = (step * 3 + kind) * ROWS
                for o in range(WLO):
                    tile = spread[at : at + ROWS, o * LANES : (o + 1) * LANES]
                    tile = jnp.where(allowed, tile, -1e30)
                    bias[
                        1 - o // HALF_LO,
                        half,
                        kind,
                        pl.ds(step * HALF_LO + o % HALF_LO, HEADS, stride=PITCH),
                        :,
                    ] = tile[:HEADS]

    loads[3].wait()
    fill_bias(1, own_chunks)

    loads[4].wait()
    for part in range(2):
        weight = qkv_ref[:, (part + 1) * features : (part + 2) * features]
        blank_rows = jnp.zeros((features - LANES, features), jnp.bfloat16)
        for slot in range(2):
            weights[part, slot, :LANES] = weight[:LANES]
            pieces = (weight[LANES:], blank_rows)
            for place in range(2):
                at = LANES + place * (features - LANES)
                weights[part, slot, at : at + features - LANES] = pieces[place ^ slot]
    queries = matmul(normed, qkv_ref[:, :features])
    head_of = lax.broadcasted_iota(jnp.int32, (PITCH, features), 1) // (features // HEADS)
    for octant in range(8):
        rows = queries[octant * PITCH : (octant + 1) * PITCH]
        stacked[octant // 4, octant % 4] = jnp.concatenate(
            [jnp.where(head_of == head, rows, 0.0) for head in range(HEADS)], axis=0
        ).astype(jnp.bfloat16)

    def project(column):
        plain = jnp.concatenate([cells[column, 0], cells[column, 2]], axis=1)
        paired = jnp.concatenate(
            [
                jnp.concatenate([cells[column, 1], cells[column, 2]], axis=1),
                jnp.concatenate([cells[column, 3], cells[column, 4]], axis=1),
            ],
            axis=0,
        )
        for part, kept in enumerate((keys, values)):
            kept[column, :LATS] = matmul(plain, weights[part, 0]).astype(jnp.bfloat16)
            kept[column, LATS:] = matmul(paired, weights[part, 1]).astype(jnp.bfloat16)

    def receive(phase, part):
        for at, (_, lat_from, lat_to, rows) in enumerate(moves):
            kinds = (tail_kinds, plain_kind)[part]
            remote(
                cells.at[1:2, kinds, pl.ds(lat_from, rows), :],
                cells.at[pl.ds(3 * phase, 1), kinds, pl.ds(lat_to, rows), :],
                phase * per_side + at * 2 + part,
                partner,
            ).wait_recv()

    def relay(phase):
        receive(phase, 0)
        pass_on(pl.ds(3 * phase, 1), phase).start()

    def gather(phase):
        receive(phase, 1)
        pass_on(pl.ds(3 * phase, 1), phase).wait_recv()
        project(3 * phase)

    at_wrap = first_lon | last_lon
    near = jnp.where(last_lon, 0, 1)
    for copy in row_copies:
        copy.wait_recv()
    own_pass.start()
    relay(near)
    pl.when(jnp.logical_not(at_wrap))(lambda: relay(1 - near))
    table_copy.wait_recv()
    fill_bias(0, chunks_in[...].astype(jnp.float32))
    own_pass.wait_recv()
    for column in (1, 2):
        project(column)
    for load in loads[5:]:
        load.wait()

    scale = (features // HEADS) ** (-0.5)
    rest = jnp.zeros((LANES - LATS, features), jnp.bfloat16)

    def window_rows(held_rows, phase, slot, half):
        at = slot * LATS + half * SIDE
        pieces = [held_rows[2 * phase + side, at : at + SIDE, :] for side in range(2)]
        return pieces + [rest]

    def attend(phases):
        octants = [(p, slot, half) for p in phases for slot in range(2) for half in range(2)]
        slot_keys = ((0,), (1, 2))

        def window(held_rows, phase, slot, half):
            return jnp.concatenate(
                [r for s in slot_keys[slot] for r in window_rows(held_rows, phase, s, half)], axis=0
            )

        scores = [
            lax.dot_general(
                stacked[phase, slot * 2 + half],
                window(keys, phase, slot, half),
                (((1,), (1,)), ((), ())),
                preferred_element_type=jnp.float32,
            )
            for phase, slot, half in octants
        ]
        shares, totals = [], []
        for (phase, slot, half), products in zip(octants, scores):
            added = jnp.concatenate([bias[phase, half, s] for s in slot_keys[slot]], axis=1)
            products = products * scale + added
            weight = jnp.exp(products - jnp.max(products, axis=-1, keepdims=True))
            shares.append(weight.astype(jnp.bfloat16))
            totals.append(jnp.sum(weight, axis=-1, keepdims=True))
        mixes = [
            matmul(weight, window(values, phase, slot, half))
            for (phase, slot, half), weight in zip(octants, shares)
        ]
        found = []
        for mixed, total in zip(mixes, totals):
            mixed = mixed * (1.0 / total)
            found.append(
                sum(
                    jnp.where(head_of == head, mixed[head * PITCH : (head + 1) * PITCH], 0.0)
                    for head in range(HEADS)
                )
            )
        context = jnp.concatenate(found, axis=0).astype(jnp.bfloat16)
        tokens = jnp.concatenate([own[p].reshape(4 * PITCH, features) for p in phases], axis=0)
        first = tokens + matmul(context, proj_ref[...])
        normed_two = layer_norm(first, gain2_ref[...]).astype(jnp.bfloat16)
        hidden = matmul(normed_two, fc1_ref[...])
        hidden = 0.5 * hidden * (1.0 + lax.erf(hidden * np.float32(0.5**0.5)))
        blended = first + lax.dot_general(
            hidden.astype(jnp.bfloat16),
            fc2_ref[...],
            (((1,), (1,)), ((), ())),
            preferred_element_type=jnp.float32,
        )
        for place, phase in enumerate(phases):
            at = place * 2 * SIDE
            rows_out[place] = blended[at : at + 2 * SIDE].reshape(2, SIDE, features)
            for a in range(WLA):
                for o in range(HALF_LO):
                    row = octant_row(a, o)
                    out_ref[a, phase * HALF_LO + o] = jnp.concatenate(
                        [rows_out[place, slot, row : row + 1, :] for slot in slots], axis=0
                    ).astype(jnp.bfloat16)

    @pl.when(first_lon)
    def _():
        pl.semaphore_wait(ready, wrapped)
        start_side(-1)

    def run_phase(step, _):
        phase = jnp.where(step == 0, near, 1 - near)
        pl.when(step == 1)(lambda: relay(phase))
        gather(phase)
        attend((phase,))
        return 0

    @pl.when(at_wrap)
    def _():
        lax.fori_loop(0, 2, run_phase, 0)

    @pl.when(jnp.logical_not(at_wrap))
    def _():
        gather(1)
        gather(0)
        attend((0, 1))

    for lon_step in (1, -1):
        for copy in first_parts[lon_step] + last_parts[lon_step]:
            copy.wait_send()
    for copy in row_copies + [own_pass, table_copy]:
        copy.wait_send()
    for phase in range(2):
        pass_on(slice(3 * phase, 3 * phase + 1), phase).wait_send()


def per_device(
    sizes,
    tokens,
    norm1_gain,
    qkv_weight,
    proj_weight,
    earth_bias,
    norm2_gain,
    fc1_weight,
    fc2_weight,
):
    assert tokens.shape[:3] == (WLV, WLA, WLO)
    assert sizes[0] == 2 and earth_bias.shape[0] == 2
    features = tokens.shape[-1]
    assert LANES + LANES // 2 == features
    operands = (
        tokens.transpose(1, 2, 0, 3),
        norm1_gain.reshape(1, -1),
        earth_bias.transpose(1, 2, 0, 3),
        jnp.asarray(toeplitz_matrix(), jnp.bfloat16),
        qkv_weight,
        proj_weight,
        norm2_gain.reshape(1, -1),
        fc1_weight,
        fc2_weight.T,
    )
    assert len(operands) == OPERANDS
    blended = pl.pallas_call(
        functools.partial(kernel, sizes),
        out_shape=jax.ShapeDtypeStruct(operands[0].shape, jnp.bfloat16),
        in_specs=[pl.BlockSpec(memory_space=pltpu.HBM)] * OPERANDS,
        out_specs=pl.BlockSpec(memory_space=pltpu.VMEM),
        scratch_shapes=[
            *[pltpu.VMEM(operand.shape, operand.dtype) for operand in operands],
            pltpu.VMEM((2, 2, SIDE, features), jnp.float32),
            pltpu.VMEM((4, KINDS, LATS, LANES), jnp.bfloat16),
            pltpu.VMEM((WLV, ROWS, earth_bias.shape[-1]), jnp.float32),
            pltpu.VMEM((3 * ROWS, SECTION), jnp.bfloat16),
            pltpu.VMEM((3 * ROWS, SECTION), jnp.bfloat16),
            pltpu.VMEM((2, 2, 3, STACK, LANES), jnp.float32),
            pltpu.VMEM((2, 2, 2 * LANES, features), jnp.bfloat16),
            pltpu.VMEM((2, 4, STACK, features), jnp.bfloat16),
            pltpu.VMEM((4, 3 * LATS, features), jnp.bfloat16),
            pltpu.VMEM((4, 3 * LATS, features), jnp.bfloat16),
            pltpu.VMEM((2, 2, SIDE, features), jnp.float32),
            pltpu.SemaphoreType.DMA((2, message_count(sizes))),
            pltpu.SemaphoreType.DMA((OPERANDS,)),
            pltpu.SemaphoreType.REGULAR,
        ],
        compiler_params=pltpu.CompilerParams(
            collective_id=0, has_side_effects=True, vmem_limit_bytes=48 * 1024 * 1024
        ),
    )(*[pltpu.with_memory_space_constraint(x, pltpu.HBM) for x in operands])
    return blended.transpose(2, 0, 1, 3)


def solution(mesh):
    placed = (
        P("lev", "lat", "lon", None),
        P(),
        P(),
        P(),
        P(None, "lat", None, None),
        P(),
        P(),
        P(),
    )
    return jax.shard_map(
        functools.partial(per_device, tuple(mesh.shape[axis] for axis in AXES)),
        mesh=mesh,
        in_specs=placed,
        out_specs=P("lev", "lat", "lon", None),
        check_vma=False,
    )
```

profile of v0, /device:TPU:27, one launch (start us, length us, event | category | flops | bytes accessed | tf_op | source)
XLA Modules:
  0.0 13.5 jit_solution(3293574746400038395)
XLA Ops:
  0.0 12.9 %shard_map.91 = bf16[6,12,2,192]{3,2,1,0:T(2,128)(2,1)S(1)} custom-call(bf16[6,12,2,192]{3,2,1,0:T(2,128)(2,1)} %bitcast.9, f32[1,192]{1,0:T(1,128)} %bitcast.10, bf16[1,6,2,3312]{3,2,1,0:T(2,128)(2,1)} %bitcast.8, bf16[138,1536]{1,0:T(8,128)(2,1)} %constant.2.clone.refs_3_, bf16[192,576]{1,0:T(8,128)(2,1)} %refs_4_.1, bf16[192,192]{1,0:T(8,128)(2,1)} %refs_5_.1, ...), custom_call_target="tpu_custom_call" | custom-call | tf_op jit(solution)/shard_map/pallas_call | solution.py:497
  12.9 0.6 %copy.11 = bf16[2,6,12,192]{3,0,2,1:T(2,128)(2,1)} copy(bf16[2,6,12,192]{3,0,2,1:T(2,128)(2,1)S(1)} %bitcast.6) | data formatting | bytes 110592
where the time goes:
time: 13.7 us; the launch traced here: 13.5 us
  Pallas kernels  12.9 us (94%)
  local copies, waits for them, and re-layouts  0.64 us (5%)
    pallas_call x1, Pallas kernels, per_device(): pl.pallas_call(functools.partial(kernel, sizes), out_shape=jax.ShapeDtype...  12.9 us
    unnamed x1, local copies, waits for them, and re-layouts  0.64 us

commit v1 on v0

--- a/solution.py
+++ b/solution.py
@@ -57,12 +57,10 @@
 
 
 def lat_moves(size, at):
-    stay = (0, PITCH, PITCH, SIDE)
+    stay = (0, 1, 1, 2)
     if size == 2:
-        source = pl.multiple_of((2 - at) * PITCH, PITCH)
-        target = pl.multiple_of(at * 3 * PITCH, PITCH)
-        return (stay, (1, source, target, PITCH))
-    return (stay, (1, 2 * PITCH, 0, PITCH), (-1, PITCH, 3 * PITCH, PITCH))
+        return (stay, (1, 2 - at, 3 * at, 1))
+    return (stay, (1, 2, 0, 1), (-1, 1, 3, 1))
 
 
 def lon_moves():
@@ -75,7 +73,7 @@
 
 def message_count(sizes):
     lats = len(lat_moves(sizes[1], 0))
-    return 4 * lats + (lats - 1) + 3 + 1
+    return 4 * lats + (lats - 1) + 3 + 1 + lats
 
 
 def kernel(sizes, *refs):
@@ -136,46 +134,69 @@
             device_id_type=pl.DeviceIdType.MESH,
         )
 
-    tail_kinds, plain_kind = slice(1, 3), slice(0, 1)
+    def part_of(columns, kinds, octants):
+        return cells.at[columns, kinds, octants, 0:OCT, :]
+
+    tail_kinds, plain_kind, passed_kinds = slice(1, 3), slice(0, 1), slice(3, 5)
     first_parts, last_parts, peers = {}, {}, {}
     for side, (lon_step, lon_from, lon_to) in enumerate(lon_moves()[:2]):
         first_parts[lon_step], last_parts[lon_step], peers[lon_step] = [], [], []
-        for at, (lat_step, lat_from, lat_to, rows) in enumerate(moves):
+        for at, (lat_step, lat_from, lat_to, octants) in enumerate(moves):
             there = device((0, lat_step, lon_step))
             peers[lon_step].append(there)
             for part, kinds in enumerate((tail_kinds, plain_kind)):
                 (first_parts, last_parts)[part][lon_step].append(
                     remote(
-                        cells.at[lon_from, kinds, pl.ds(lat_from, rows), :],
-                        cells.at[lon_to, kinds, pl.ds(lat_to, rows), :],
+                        part_of(lon_from, kinds, pl.ds(lat_from, octants)),
+                        part_of(lon_to, kinds, pl.ds(lat_to, octants)),
                         side * per_side + at * 2 + part,
                         there,
                     )
                 )
     row_copies, row_peers = [], []
-    for at, (lat_step, lat_from, lat_to, rows) in enumerate(moves[1:]):
+    for at, (lat_step, lat_from, lat_to, octants) in enumerate(moves[1:]):
         row_peers.append(device((0, lat_step, 0)))
         row_copies.append(
             remote(
-                cells.at[1:3, 0:3, pl.ds(lat_from, rows), :],
-                cells.at[1:3, 0:3, pl.ds(lat_to, rows), :],
+                part_of(slice(1, 3), slice(0, 3), pl.ds(lat_from, octants)),
+                part_of(slice(1, 3), slice(0, 3), pl.ds(lat_to, octants)),
                 2 * per_side + at,
                 row_peers[-1],
             )
         )
     partner = device((1, 0, 0))
     passed = 2 * per_side + len(row_copies)
+    used = pl.ds(1 - lat, 3) if sizes[1] == 2 else slice(0, 4)
 
     def pass_on(columns, index):
         return remote(
-            cells.at[columns, 1:3, :, :], cells.at[columns, 3:5, :, :], passed + index, partner
+            part_of(columns, tail_kinds, used),
+            part_of(columns, passed_kinds, used),
+            passed + index,
+            partner,
         )
 
     own_pass = pass_on(slice(1, 3), 2)
     table_copy = remote(chunks_out, chunks_in, passed + 3, device((0, 1, 0)))
+    crossings, cross_peers = {}, {}
+    for lon_step, lon_from, lon_to in lon_moves()[:2]:
+        crossings[lon_step], cross_peers[lon_step] = [], []
+        for at, (lat_step, lat_from, lat_to, octants) in enumerate(moves):
+            there = device((1, lat_step, lon_step))
+            cross_peers[lon_step].append(there)
+            crossings[lon_step].append(
+                remote(
+                    part_of(lon_from, tail_kinds, pl.ds(lat_from, octants)),
+                    part_of(lon_to, passed_kinds, pl.ds(lat_to, octants)),
+                    passed + 4 + at,
+                    there,
+                )
+            )
 
     barrier = pltpu.get_barrier_semaphore()
     first_lon, last_lon = lon == 0, lon == sizes[2] - 1
+    before_last = lon == sizes[2] - 2
+    at_wrap = first_lon | last_lon
 
     def tell(semaphore, group):
         for there in group:
@@ -183,26 +204,40 @@
                 semaphore, inc=1, device_id=there, device_id_type=pl.DeviceIdType.MESH
             )
 
-    tell(barrier, row_peers + [partner] + peers[-1])
-    pl.when(jnp.logical_not(last_lon))(lambda: tell(barrier, peers[1]))
+    def start(*groups):
+        for group in groups:
+            for copy in group:
+                copy.start()
+
     wrapped = len(moves)
     greetings = len(row_peers) + 1 + 2 * wrapped
-
-    for start in (OCT, PITCH + OCT):
-        own[:, :, start : start + PITCH - OCT, :] = jnp.zeros(
+    tell(barrier, peers[-1])
+    pl.when(first_lon)(lambda: tell(barrier, cross_peers[-1]))
+    pl.when(last_lon)(lambda: tell(barrier, [device((1, 0, -1))]))
+    pl.when(jnp.logical_not(last_lon))(lambda: tell(barrier, row_peers + [partner]))
+    pl.when(jnp.logical_not(last_lon | before_last))(lambda: tell(barrier, peers[1]))
+
+    cells[:, :, :, OCT:, :] = jnp.zeros((4, KINDS, 4, PITCH - OCT, LANES), jnp.bfloat16)
+    for pad in (OCT, PITCH + OCT):
+        own[:, :, pad : pad + PITCH - OCT, :] = jnp.zeros(
             (2, 2, PITCH - OCT, features), jnp.float32
         )
     if sizes[1] == 2:
-        blank = jnp.zeros((4, 3, PITCH, LANES), jnp.bfloat16)
+        blank = jnp.zeros((4, KINDS, PITCH, LANES), jnp.bfloat16)
 
         def clear_low():
-            cells[:, 0:3, :PITCH, :] = blank
+            cells[:, :, 0] = blank
 
         def clear_high():
-            cells[:, 0:3, 3 * PITCH :, :] = blank
+            cells[:, :, 3] = blank
 
         pl.when(lat == 0)(clear_low)
         pl.when(lat == 1)(clear_high)
+
+    @pl.when(last_lon)
+    def _():
+        pl.semaphore_wait(barrier, 2 * wrapped)
+        tell(ready, peers[1] + cross_peers[1])
 
     loads[0].wait()
     for a in range(WLA):
@@ -218,40 +253,37 @@
         paired = normed[half * 2 * SIDE + SIDE : (half + 1) * 2 * SIDE]
         tails = jnp.concatenate([plain[:, LANES:], paired[:, LANES:]], axis=1)
         for kind, block in enumerate((plain[:, :LANES], paired[:, :LANES], tails)):
-            cells[1 + half, kind, PITCH : PITCH + SIDE, :] = block.astype(jnp.bfloat16)
+            cells[1 + half, kind, 1:3] = block.reshape(2, PITCH, LANES).astype(jnp.bfloat16)
     normed = normed.astype(jnp.bfloat16)
-    pl.semaphore_wait(barrier, jnp.where(first_lon, greetings - wrapped, greetings))
-
-    def start(*groups):
-        for group in groups:
-            for copy in group:
-                copy.start()
-
-    def start_side(lon_step):
-        start(first_parts[lon_step], last_parts[lon_step])
-
-    @pl.when(last_lon)
+
+    def over_wrap(lon_step, at_lat, at_lev):
+        own = [first_parts[lon_step], last_parts[lon_step]]
+        for to_lat in range(2):
+            index = at_lat ^ to_lat
+            groups = [own, [crossings[lon_step]]]
+            for group in groups[at_lev], groups[1 - at_lev]:
+                for copies in group:
+                    copies[index].start()
+
+    def send_over_wrap(lon_step, order):
+        if sizes[1] != 2:
+            start(first_parts[lon_step], last_parts[lon_step], crossings[lon_step])
+            return
+        for at_lat in range(2):
+            for at_lev in range(2):
+                pl.when((lat == at_lat) & (lev == at_lev))(
+                    functools.partial(over_wrap, lon_step, at_lat, at_lev ^ order)
+                )
+
+    pl.when(last_lon)(lambda: send_over_wrap(1, 0))
+
+    @pl.when(jnp.logical_not(last_lon))
     def _():
-        if sizes[1] == 2:
-            for at_lat in range(2):
-
-                @pl.when(lat == at_lat)
-                def _(at_lat=at_lat):
-                    for to_lat in range(2):
-                        first_parts[1][at_lat ^ to_lat].start()
-                        last_parts[1][at_lat ^ to_lat].start()
-        else:
-            start_side(1)
-        tell(ready, peers[1])
-        start_side(-1)
-
-    pl.when(first_lon)(lambda: start_side(1))
-
-    @pl.when(jnp.logical_not(first_lon | last_lon))
-    def _():
-        start(first_parts[1], first_parts[-1], last_parts[1], last_parts[-1])
-
-    start(row_copies)
+        expected = jnp.where(first_lon, greetings - wrapped, greetings)
+        pl.semaphore_wait(barrier, jnp.where(before_last, greetings + 1, expected))
+        pl.when(before_last)(lambda: tell(ready, peers[1]))
+        pl.when(jnp.logical_not(first_lon))(lambda: start(first_parts[-1], last_parts[-1]))
+        start(row_copies, first_parts[1], last_parts[1])
 
     loads[2].wait()
     tables[...] = jnp.zeros_like(tables)
@@ -272,7 +304,7 @@
         return jnp.concatenate(found, axis=0)
 
     chunks_out[...] = sections(1).astype(jnp.bfloat16)
-    table_copy.start()
+    pl.when(jnp.logical_not(last_lon))(table_copy.start)
     own_chunks = sections(0)
 
     lane = lax.broadcasted_iota(jnp.int32, (ROWS, LANES), 1)
@@ -322,11 +354,14 @@
         ).astype(jnp.bfloat16)
 
     def project(column):
-        plain = jnp.concatenate([cells[column, 0], cells[column, 2]], axis=1)
+        plain, paired, tails, passed_on, passed_tails = (
+            cells[column, kind].reshape(LATS, LANES) for kind in range(KINDS)
+        )
+        plain = jnp.concatenate([plain, tails], axis=1)
         paired = jnp.concatenate(
             [
-                jnp.concatenate([cells[column, 1], cells[column, 2]], axis=1),
-                jnp.concatenate([cells[column, 3], cells[column, 4]], axis=1),
+                jnp.concatenate([paired, tails], axis=1),
+                jnp.concatenate([passed_on, passed_tails], axis=1),
             ],
             axis=0,
         )
@@ -335,11 +370,11 @@
             kept[column, LATS:] = matmul(paired, weights[part, 1]).astype(jnp.bfloat16)
 
     def receive(phase, part):
-        for at, (_, lat_from, lat_to, rows) in enumerate(moves):
+        for at, (_, lat_from, lat_to, octants) in enumerate(moves):
             kinds = (tail_kinds, plain_kind)[part]
             remote(
-                cells.at[1:2, kinds, pl.ds(lat_from, rows), :],
-                cells.at[pl.ds(3 * phase, 1), kinds, pl.ds(lat_to, rows), :],
+                part_of(slice(1, 2), kinds, pl.ds(lat_from, octants)),
+                part_of(pl.ds(3 * phase, 1), kinds, pl.ds(lat_to, octants)),
                 phase * per_side + at * 2 + part,
                 partner,
             ).wait_recv()
@@ -348,13 +383,16 @@
         receive(phase, 0)
         pass_on(pl.ds(3 * phase, 1), phase).start()
 
-    def gather(phase):
-        receive(phase, 1)
+    def relayed(phase):
         pass_on(pl.ds(3 * phase, 1), phase).wait_recv()
-        project(3 * phase)
-
-    at_wrap = first_lon | last_lon
+
     near = jnp.where(last_lon, 0, 1)
+
+    @pl.when(last_lon)
+    def _():
+        pl.semaphore_wait(ready, wrapped)
+        start(row_copies, [table_copy], first_parts[-1], last_parts[-1])
+
     for copy in row_copies:
         copy.wait_recv()
     own_pass.start()
@@ -438,33 +476,46 @@
 
     @pl.when(first_lon)
     def _():
-        pl.semaphore_wait(ready, wrapped)
-        start_side(-1)
+        pl.semaphore_wait(ready, 2 * wrapped)
+        send_over_wrap(-1, 1)
 
     def run_phase(step, _):
         phase = jnp.where(step == 0, near, 1 - near)
-        pl.when(step == 1)(lambda: relay(phase))
-        gather(phase)
+        pl.when(step == 0)(lambda: relayed(phase))
+
+        @pl.when(step == 1)
+        def _():
+            receive(phase, 0)
+            for copy in crossings[1]:
+                copy.wait_recv()
+
+        receive(phase, 1)
+        project(3 * phase)
         attend((phase,))
         return 0
 
     @pl.when(at_wrap)
     def _():
         lax.fori_loop(0, 2, run_phase, 0)
+        pass_on(pl.ds(3 * near, 1), near).wait_send()
+        for copy in crossings[1]:
+            copy.wait_send()
 
     @pl.when(jnp.logical_not(at_wrap))
     def _():
-        gather(1)
-        gather(0)
+        for phase in (1, 0):
+            receive(phase, 1)
+            relayed(phase)
+            project(3 * phase)
         attend((0, 1))
+        for phase in range(2):
+            pass_on(slice(3 * phase, 3 * phase + 1), phase).wait_send()
 
     for lon_step in (1, -1):
         for copy in first_parts[lon_step] + last_parts[lon_step]:
             copy.wait_send()
     for copy in row_copies + [own_pass, table_copy]:
         copy.wait_send()
-    for phase in range(2):
-        pass_on(slice(3 * phase, 3 * phase + 1), phase).wait_send()
 
 
 def per_device(
@@ -479,7 +530,7 @@
     fc2_weight,
 ):
     assert tokens.shape[:3] == (WLV, WLA, WLO)
-    assert sizes[0] == 2 and earth_bias.shape[0] == 2
+    assert sizes[0] == 2 and sizes[2] > 3 and earth_bias.shape[0] == 2
     features = tokens.shape[-1]
     assert LANES + LANES // 2 == features
     operands = (
@@ -502,7 +553,7 @@
         scratch_shapes=[
             *[pltpu.VMEM(operand.shape, operand.dtype) for operand in operands],
             pltpu.VMEM((2, 2, SIDE, features), jnp.float32),
-            pltpu.VMEM((4, KINDS, LATS, LANES), jnp.bfloat16),
+            pltpu.VMEM((4, KINDS, 4, PITCH, LANES), jnp.bfloat16),
             pltpu.VMEM((WLV, ROWS, earth_bias.shape[-1]), jnp.float32),
             pltpu.VMEM((3 * ROWS, SECTION), jnp.bfloat16),
             pltpu.VMEM((3 * ROWS, SECTION), jnp.bfloat16),

time: 13.7 us -> 12.4 us (0.905)
  the two profiles are of different devices: /device:TPU:27 before, /device:TPU:0 now
where the time goes in v1:
time: 12.4 us; the launch traced here: 12.2 us
  Pallas kernels  11.6 us (94%)
  local copies, waits for them, and re-layouts  0.64 us (5%)
    pallas_call x1, Pallas kernels, per_device(): pl.pallas_call(functools.partial(kernel, sizes), out_shape=jax.ShapeDtype...  11.6 us
    unnamed x1, local copies, waits for them, and re-layouts  0.64 us

profile of v1, /device:TPU:0, one launch (start us, length us, event | category | flops | bytes accessed | tf_op | source)
XLA Modules:
  0.0 12.2 jit_solution(17384071359352165203)
XLA Ops:
  0.0 11.6 %shard_map.91 = bf16[6,12,2,192]{3,2,1,0:T(2,128)(2,1)S(1)} custom-call(bf16[6,12,2,192]{3,2,1,0:T(2,128)(2,1)} %bitcast.9, f32[1,192]{1,0:T(1,128)} %bitcast.10, bf16[1,6,2,3312]{3,2,1,0:T(2,128)(2,1)} %bitcast.8, bf16[138,1536]{1,0:T(8,128)(2,1)} %constant.2.clone.refs_3_, bf16[192,576]{1,0:T(8,128)(2,1)} %refs_4_.1, bf16[192,192]{1,0:T(8,128)(2,1)} %refs_5_.1, ...), custom_call_target="tpu_custom_call" | custom-call | tf_op jit(solution)/shard_map/pallas_call | solution.py:548
  11.6 0.6 %copy.11 = bf16[2,6,12,192]{3,0,2,1:T(2,128)(2,1)} copy(bf16[2,6,12,192]{3,0,2,1:T(2,128)(2,1)S(1)} %bitcast.6) | data formatting | bytes 110592

commit v2 on v1

--- a/solution.py
+++ b/solution.py
@@ -45,13 +45,6 @@
     return pick
 
 
-def layer_norm(values, scale_gain):
-    average = jnp.mean(values, axis=-1, keepdims=True)
-    centered = values - average
-    variance = jnp.mean(centered * centered, axis=-1, keepdims=True)
-    return centered * lax.rsqrt(variance + norm_eps) * scale_gain
-
-
 def matmul(a, b):
     return jnp.dot(a, b, preferred_element_type=jnp.float32)
 
@@ -77,7 +70,7 @@
 
 
 def kernel(sizes, *refs):
-    operands, out_ref, held = refs[:OPERANDS], refs[OPERANDS], refs[OPERANDS + 1 : -14]
+    operands, out_ref, held = refs[:OPERANDS], refs[OPERANDS], refs[OPERANDS + 1 : -15]
     (
         own,
         cells,
@@ -93,7 +86,8 @@
         sems,
         load_sems,
         ready,
-    ) = refs[-14:]
+        means,
+    ) = refs[-15:]
     loads = [
         pltpu.make_async_copy(source, place, load_sems.at[i])
         for i, (source, place) in enumerate(zip(operands, held))
@@ -247,12 +241,21 @@
             for side in range(WLV):
                 own[o // HALF_LO, slots[side], row : row + 1, :] = cell[side : side + 1]
     loads[1].wait()
-    normed = layer_norm(own[...].reshape(4 * SIDE, features), gain1_ref[...])
+    raw = own[...].reshape(4 * SIDE, features)
+    averages = jnp.mean(raw, axis=-1, keepdims=True)
+    normed = raw - averages
+    scales = lax.rsqrt(jnp.mean(normed * normed, axis=-1, keepdims=True) + norm_eps)
+    normed = normed * scales * gain1_ref[...]
+    lower = lax.broadcasted_iota(jnp.int32, (SIDE, LANES), 1) < features - LANES
+    tail_gain = jnp.concatenate([gain1_ref[:, LANES:]] * 2, axis=1)
     for half in range(2):
-        plain = normed[half * 2 * SIDE : half * 2 * SIDE + SIDE]
-        paired = normed[half * 2 * SIDE + SIDE : (half + 1) * 2 * SIDE]
-        tails = jnp.concatenate([plain[:, LANES:], paired[:, LANES:]], axis=1)
-        for kind, block in enumerate((plain[:, :LANES], paired[:, :LANES], tails)):
+        pair = [slice(at, at + SIDE) for at in (half * 2 * SIDE, (half * 2 + 1) * SIDE)]
+        tails = jnp.concatenate([raw[rows, LANES:] for rows in pair], axis=1)
+        average, by = (
+            jnp.where(lower, found[pair[0]], found[pair[1]]) for found in (averages, scales)
+        )
+        tails = (tails - average) * by * tail_gain
+        for kind, block in enumerate((normed[pair[0], :LANES], normed[pair[1], :LANES], tails)):
             cells[1 + half, kind, 1:3] = block.reshape(2, PITCH, LANES).astype(jnp.bfloat16)
     normed = normed.astype(jnp.bfloat16)
 
@@ -396,6 +399,11 @@
     for copy in row_copies:
         copy.wait_recv()
     own_pass.start()
+    @pl.when(first_lon)
+    def _():
+        pl.semaphore_wait(ready, 2 * wrapped)
+        send_over_wrap(-1, 1)
+
     relay(near)
     pl.when(jnp.logical_not(at_wrap))(lambda: relay(1 - near))
     table_copy.wait_recv()
@@ -405,6 +413,11 @@
         project(column)
     for load in loads[5:]:
         load.wait()
+    row_mean = jnp.mean(proj_ref[...].astype(jnp.float32), axis=-1, keepdims=True)
+    high_part = row_mean.astype(jnp.bfloat16)
+    low_part = (row_mean - high_part.astype(jnp.float32)).astype(jnp.bfloat16)
+    for part, column in enumerate((high_part, low_part)):
+        means[:, part * LANES : (part + 1) * LANES] = jnp.broadcast_to(column, (features, LANES))
 
     scale = (features // HEADS) ** (-0.5)
     rest = jnp.zeros((LANES - LATS, features), jnp.bfloat16)
@@ -454,8 +467,14 @@
             )
         context = jnp.concatenate(found, axis=0).astype(jnp.bfloat16)
         tokens = jnp.concatenate([own[p].reshape(4 * PITCH, features) for p in phases], axis=0)
+        average = matmul(context, means[...])
+        average = average[:, :LANES] + average[:, LANES:]
+        average = average + jnp.mean(tokens, axis=-1, keepdims=True)
         first = tokens + matmul(context, proj_ref[...])
-        normed_two = layer_norm(first, gain2_ref[...]).astype(jnp.bfloat16)
+        centered = first - jnp.concatenate([average, average[:, : features - LANES]], axis=1)
+        variance = jnp.mean(centered * centered, axis=-1, keepdims=True)
+        normed_two = centered * lax.rsqrt(variance + norm_eps) * gain2_ref[...]
+        normed_two = normed_two.astype(jnp.bfloat16)
         hidden = matmul(normed_two, fc1_ref[...])
         hidden = 0.5 * hidden * (1.0 + lax.erf(hidden * np.float32(0.5**0.5)))
         blended = first + lax.dot_general(
@@ -466,18 +485,17 @@
         )
         for place, phase in enumerate(phases):
             at = place * 2 * SIDE
-            rows_out[place] = blended[at : at + 2 * SIDE].reshape(2, SIDE, features)
+            for slot in range(2):
+                rows = blended[at + slot * SIDE : at + (slot + 1) * SIDE]
+                target = pl.ds(slots[slot], SIDE, stride=2)
+                rows_out[place, 0, target, :] = rows[:, :LANES]
+                rows_out[place, 1, target, : features - LANES] = rows[:, LANES:]
             for a in range(WLA):
                 for o in range(HALF_LO):
-                    row = octant_row(a, o)
-                    out_ref[a, phase * HALF_LO + o] = jnp.concatenate(
-                        [rows_out[place, slot, row : row + 1, :] for slot in slots], axis=0
-                    ).astype(jnp.bfloat16)
-
-    @pl.when(first_lon)
-    def _():
-        pl.semaphore_wait(ready, 2 * wrapped)
-        send_over_wrap(-1, 1)
+                    row = 2 * octant_row(a, o)
+                    pieces = rows_out[place, :, row : row + 2, :].astype(jnp.bfloat16)
+                    out_ref[a, phase * HALF_LO + o, :, :LANES] = pieces[0]
+                    out_ref[a, phase * HALF_LO + o, :, LANES:] = pieces[1, :, : features - LANES]
 
     def run_phase(step, _):
         phase = jnp.where(step == 0, near, 1 - near)
@@ -562,10 +580,11 @@
             pltpu.VMEM((2, 4, STACK, features), jnp.bfloat16),
             pltpu.VMEM((4, 3 * LATS, features), jnp.bfloat16),
             pltpu.VMEM((4, 3 * LATS, features), jnp.bfloat16),
-            pltpu.VMEM((2, 2, SIDE, features), jnp.float32),
+            pltpu.VMEM((2, 2, 2 * SIDE, LANES), jnp.float32),
             pltpu.SemaphoreType.DMA((2, message_count(sizes))),
             pltpu.SemaphoreType.DMA((OPERANDS,)),
             pltpu.SemaphoreType.REGULAR,
+            pltpu.VMEM((features, 2 * LANES), jnp.bfloat16),
         ],
         compiler_params=pltpu.CompilerParams(
             collective_id=0, has_side_effects=True, vmem_limit_bytes=48 * 1024 * 1024

time: 12.4 us -> 12.3 us (level)
  no operation moved by 1% of the time
where the time goes in v2:
time: 12.3 us; the launch traced here: 12.1 us
  Pallas kernels  11.5 us (93%)
  local copies, waits for them, and re-layouts  0.64 us (5%)
    pallas_call x1, Pallas kernels, per_device(): pl.pallas_call(functools.partial(kernel, sizes), out_shape=jax.ShapeDtype...  11.5 us
    unnamed x1, local copies, waits for them, and re-layouts  0.64 us

profile of v2, /device:TPU:0, one launch (start us, length us, event | category | flops | bytes accessed | tf_op | source)
XLA Modules:
  0.0 12.1 jit_solution(14564769602130875704)
XLA Ops:
  0.0 11.5 %shard_map.91 = bf16[6,12,2,192]{3,2,1,0:T(2,128)(2,1)S(1)} custom-call(bf16[6,12,2,192]{3,2,1,0:T(2,128)(2,1)} %bitcast.9, f32[1,192]{1,0:T(1,128)} %bitcast.10, bf16[1,6,2,3312]{3,2,1,0:T(2,128)(2,1)} %bitcast.8, bf16[138,1536]{1,0:T(8,128)(2,1)} %constant.2.clone.refs_3_, bf16[192,576]{1,0:T(8,128)(2,1)} %refs_4_.1, bf16[192,192]{1,0:T(8,128)(2,1)} %refs_5_.1, ...), custom_call_target="tpu_custom_call" | custom-call | tf_op jit(solution)/shard_map/pallas_call | solution.py:566
  11.5 0.6 %copy.11 = bf16[2,6,12,192]{3,0,2,1:T(2,128)(2,1)} copy(bf16[2,6,12,192]{3,0,2,1:T(2,128)(2,1)S(1)} %bitcast.6) | data formatting | bytes 110592

commit v3 on v2

--- a/solution.py
+++ b/solution.py
@@ -88,11 +88,18 @@
         ready,
         means,
     ) = refs[-15:]
-    loads = [
-        pltpu.make_async_copy(source, place, load_sems.at[i])
-        for i, (source, place) in enumerate(zip(operands, held))
+    token_loads = [
+        pltpu.make_async_copy(
+            operands[0].at[pl.ds(side * HALF_LA, HALF_LA)],
+            held[0].at[pl.ds(side * HALF_LA, HALF_LA)],
+            load_sems.at[side * OPERANDS],
+        )
+        for side in range(2)
     ]
-    for load in loads:
+    loads = token_loads[:1] + [
+        pltpu.make_async_copy(operands[i], held[i], load_sems.at[i]) for i in range(1, OPERANDS)
+    ]
+    for load in token_loads + loads[1:]:
         load.start()
     (
         tokens_ref,
@@ -233,8 +240,9 @@
         pl.semaphore_wait(barrier, 2 * wrapped)
         tell(ready, peers[1] + cross_peers[1])
 
-    loads[0].wait()
     for a in range(WLA):
+        if a % HALF_LA == 0:
+            token_loads[a // HALF_LA].wait()
         for o in range(WLO):
             cell = tokens_ref[a, o].astype(jnp.float32)
             row = octant_row(a, o)
@@ -582,7 +590,7 @@
             pltpu.VMEM((4, 3 * LATS, features), jnp.bfloat16),
             pltpu.VMEM((2, 2, 2 * SIDE, LANES), jnp.float32),
             pltpu.SemaphoreType.DMA((2, message_count(sizes))),
-            pltpu.SemaphoreType.DMA((OPERANDS,)),
+            pltpu.SemaphoreType.DMA((OPERANDS + 1,)),
             pltpu.SemaphoreType.REGULAR,
             pltpu.VMEM((features, 2 * LANES), jnp.bfloat16),
         ],

time: 12.3 us -> 12.2 us (level)
  no operation moved by 1% of the time
where the time goes in v3:
time: 12.2 us; the launch traced here: 12 us
  Pallas kernels  11.4 us (93%)
  local copies, waits for them, and re-layouts  0.64 us (5%)
    pallas_call x1, Pallas kernels, per_device(): pl.pallas_call(functools.partial(kernel, sizes), out_shape=jax.ShapeDtype...  11.4 us
    unnamed x1, local copies, waits for them, and re-layouts  0.64 us

profile of v3, /device:TPU:0, one launch (start us, length us, event | category | flops | bytes accessed | tf_op | source)
XLA Modules:
  0.0 12.0 jit_solution(7948138324632596131)
XLA Ops:
  0.0 11.4 %shard_map.91 = bf16[6,12,2,192]{3,2,1,0:T(2,128)(2,1)S(1)} custom-call(bf16[6,12,2,192]{3,2,1,0:T(2,128)(2,1)} %bitcast.9, f32[1,192]{1,0:T(1,128)} %bitcast.10, bf16[1,6,2,3312]{3,2,1,0:T(2,128)(2,1)} %bitcast.8, bf16[138,1536]{1,0:T(8,128)(2,1)} %constant.2.clone.refs_3_, bf16[192,576]{1,0:T(8,128)(2,1)} %refs_4_.1, bf16[192,192]{1,0:T(8,128)(2,1)} %refs_5_.1, ...), custom_call_target="tpu_custom_call" | custom-call | tf_op jit(solution)/shard_map/pallas_call | solution.py:574
  11.4 0.6 %copy.11 = bf16[2,6,12,192]{3,0,2,1:T(2,128)(2,1)} copy(bf16[2,6,12,192]{3,0,2,1:T(2,128)(2,1)S(1)} %bitcast.6) | data formatting | bytes 110592

commit v4 on v3

--- a/solution.py
+++ b/solution.py
@@ -27,6 +27,7 @@
 STACK = HEADS * PITCH
 SECTION = HALF_LA * CHUNK
 KINDS = 5
+LOAD_ROWS = 2
 
 norm_eps = 1e-05
 
@@ -90,11 +91,11 @@
     ) = refs[-15:]
     token_loads = [
         pltpu.make_async_copy(
-            operands[0].at[pl.ds(side * HALF_LA, HALF_LA)],
-            held[0].at[pl.ds(side * HALF_LA, HALF_LA)],
-            load_sems.at[side * OPERANDS],
-        )
-        for side in range(2)
+            operands[0].at[pl.ds(part * LOAD_ROWS, LOAD_ROWS)],
+            held[0].at[pl.ds(part * LOAD_ROWS, LOAD_ROWS)],
+            load_sems.at[OPERANDS - 1 + part if part else 0],
+        )
+        for part in range(WLA // LOAD_ROWS)
     ]
     loads = token_loads[:1] + [
         pltpu.make_async_copy(operands[i], held[i], load_sems.at[i]) for i in range(1, OPERANDS)
@@ -241,8 +242,8 @@
         tell(ready, peers[1] + cross_peers[1])
 
     for a in range(WLA):
-        if a % HALF_LA == 0:
-            token_loads[a // HALF_LA].wait()
+        if a % LOAD_ROWS == 0:
+            token_loads[a // LOAD_ROWS].wait()
         for o in range(WLO):
             cell = tokens_ref[a, o].astype(jnp.float32)
             row = octant_row(a, o)
@@ -484,8 +485,8 @@
         normed_two = centered * lax.rsqrt(variance + norm_eps) * gain2_ref[...]
         normed_two = normed_two.astype(jnp.bfloat16)
         hidden = matmul(normed_two, fc1_ref[...])
-        hidden = 0.5 * hidden * (1.0 + lax.erf(hidden * np.float32(0.5**0.5)))
-        blended = first + lax.dot_general(
+        hidden = hidden * (1.0 + lax.erf(hidden * np.float32(0.5**0.5)))
+        blended = first + 0.5 * lax.dot_general(
             hidden.astype(jnp.bfloat16),
             fc2_ref[...],
             (((1,), (1,)), ((), ())),
@@ -590,7 +591,7 @@
             pltpu.VMEM((4, 3 * LATS, features), jnp.bfloat16),
             pltpu.VMEM((2, 2, 2 * SIDE, LANES), jnp.float32),
             pltpu.SemaphoreType.DMA((2, message_count(sizes))),
-            pltpu.SemaphoreType.DMA((OPERANDS + 1,)),
+            pltpu.SemaphoreType.DMA((OPERANDS - 1 + WLA // LOAD_ROWS,)),
             pltpu.SemaphoreType.REGULAR,
             pltpu.VMEM((features, 2 * LANES), jnp.bfloat16),
         ],

time: 12.2 us -> 12.1 us (level)
  no operation moved by 1% of the time
where the time goes in v4:
time: 12.1 us; the launch traced here: 12 us
  Pallas kernels  11.4 us (94%)
  local copies, waits for them, and re-layouts  0.64 us (5%)
    pallas_call x1, Pallas kernels, per_device(): pl.pallas_call(functools.partial(kernel, sizes), out_shape=jax.ShapeDtype...  11.4 us
    unnamed x1, local copies, waits for them, and re-layouts  0.64 us

profile of v4, /device:TPU:0, one launch (start us, length us, event | category | flops | bytes accessed | tf_op | source)
XLA Modules:
  0.0 12.0 jit_solution(68550074519612161)
XLA Ops:
  0.0 11.4 %shard_map.91 = bf16[6,12,2,192]{3,2,1,0:T(2,128)(2,1)S(1)} custom-call(bf16[6,12,2,192]{3,2,1,0:T(2,128)(2,1)} %bitcast.9, f32[1,192]{1,0:T(1,128)} %bitcast.10, bf16[1,6,2,3312]{3,2,1,0:T(2,128)(2,1)} %bitcast.8, bf16[138,1536]{1,0:T(8,128)(2,1)} %constant.2.clone.refs_3_, bf16[192,576]{1,0:T(8,128)(2,1)} %refs_4_.1, bf16[192,192]{1,0:T(8,128)(2,1)} %refs_5_.1, ...), custom_call_target="tpu_custom_call" | custom-call | tf_op jit(solution)/shard_map/pallas_call | solution.py:575
  11.4 0.6 %copy.11 = bf16[2,6,12,192]{3,0,2,1:T(2,128)(2,1)} copy(bf16[2,6,12,192]{3,0,2,1:T(2,128)(2,1)S(1)} %bitcast.6) | data formatting | bytes 110592

commit v5 on v4

--- a/solution.py
+++ b/solution.py
@@ -408,13 +408,13 @@
     for copy in row_copies:
         copy.wait_recv()
     own_pass.start()
+    relay(near)
+    pl.when(jnp.logical_not(at_wrap))(lambda: relay(1 - near))
     @pl.when(first_lon)
     def _():
         pl.semaphore_wait(ready, 2 * wrapped)
         send_over_wrap(-1, 1)
 
-    relay(near)
-    pl.when(jnp.logical_not(at_wrap))(lambda: relay(1 - near))
     table_copy.wait_recv()
     fill_bias(0, chunks_in[...].astype(jnp.float32))
     own_pass.wait_recv()

time: 12.1 us -> 12.1 us (level)
  no operation moved by 1% of the time
where the time goes in v5:
time: 12.1 us; the launch traced here: 12 us
  Pallas kernels  11.4 us (94%)
  local copies, waits for them, and re-layouts  0.64 us (5%)
    pallas_call x1, Pallas kernels, per_device(): pl.pallas_call(functools.partial(kernel, sizes), out_shape=jax.ShapeDtype...  11.4 us
    unnamed x1, local copies, waits for them, and re-layouts  0.64 us

profile of v5, /device:TPU:0, one launch (start us, length us, event | category | flops | bytes accessed | tf_op | source)
XLA Modules:
  0.0 12.0 jit_solution(16221135722964997300)
XLA Ops:
  0.0 11.4 %shard_map.91 = bf16[6,12,2,192]{3,2,1,0:T(2,128)(2,1)S(1)} custom-call(bf16[6,12,2,192]{3,2,1,0:T(2,128)(2,1)} %bitcast.9, f32[1,192]{1,0:T(1,128)} %bitcast.10, bf16[1,6,2,3312]{3,2,1,0:T(2,128)(2,1)} %bitcast.8, bf16[138,1536]{1,0:T(8,128)(2,1)} %constant.2.clone.refs_3_, bf16[192,576]{1,0:T(8,128)(2,1)} %refs_4_.1, bf16[192,192]{1,0:T(8,128)(2,1)} %refs_5_.1, ...), custom_call_target="tpu_custom_call" | custom-call | tf_op jit(solution)/shard_map/pallas_call | solution.py:575
  11.4 0.6 %copy.11 = bf16[2,6,12,192]{3,0,2,1:T(2,128)(2,1)} copy(bf16[2,6,12,192]{3,0,2,1:T(2,128)(2,1)S(1)} %bitcast.6) | data formatting | bytes 110592

commit v6 on v5

--- a/solution.py
+++ b/solution.py
@@ -410,14 +410,14 @@
     own_pass.start()
     relay(near)
     pl.when(jnp.logical_not(at_wrap))(lambda: relay(1 - near))
+    table_copy.wait_recv()
+    fill_bias(0, chunks_in[...].astype(jnp.float32))
+    own_pass.wait_recv()
     @pl.when(first_lon)
     def _():
         pl.semaphore_wait(ready, 2 * wrapped)
         send_over_wrap(-1, 1)
 
-    table_copy.wait_recv()
-    fill_bias(0, chunks_in[...].astype(jnp.float32))
-    own_pass.wait_recv()
     for column in (1, 2):
         project(column)
     for load in loads[5:]:

time: 12.1 us -> 12.1 us (level)
  no operation moved by 1% of the time
where the time goes in v6:
time: 12.1 us; the launch traced here: 12 us
  Pallas kernels  11.4 us (94%)
  local copies, waits for them, and re-layouts  0.64 us (5%)
    pallas_call x1, Pallas kernels, per_device(): pl.pallas_call(functools.partial(kernel, sizes), out_shape=jax.ShapeDtype...  11.4 us
    unnamed x1, local copies, waits for them, and re-layouts  0.64 us

profile of v6, /device:TPU:0, one launch (start us, length us, event | category | flops | bytes accessed | tf_op | source)
XLA Modules:
  0.0 12.0 jit_solution(5731126781723109794)
XLA Ops:
  0.0 11.4 %shard_map.91 = bf16[6,12,2,192]{3,2,1,0:T(2,128)(2,1)S(1)} custom-call(bf16[6,12,2,192]{3,2,1,0:T(2,128)(2,1)} %bitcast.9, f32[1,192]{1,0:T(1,128)} %bitcast.10, bf16[1,6,2,3312]{3,2,1,0:T(2,128)(2,1)} %bitcast.8, bf16[138,1536]{1,0:T(8,128)(2,1)} %constant.2.clone.refs_3_, bf16[192,576]{1,0:T(8,128)(2,1)} %refs_4_.1, bf16[192,192]{1,0:T(8,128)(2,1)} %refs_5_.1, ...), custom_call_target="tpu_custom_call" | custom-call | tf_op jit(solution)/shard_map/pallas_call | solution.py:575
  11.4 0.6 %copy.11 = bf16[2,6,12,192]{3,0,2,1:T(2,128)(2,1)} copy(bf16[2,6,12,192]{3,0,2,1:T(2,128)(2,1)S(1)} %bitcast.6) | data formatting | bytes 110592
